TPU v7x, 32 devices: a whole 2x2x4 slice. The times are simulated.
32 devices in a mesh: dp: 4 (over y, x), expert: 8 (over z, core).
Axes of the slice: x: 2, y: 2, z: 4, core: 2. Of those that a mesh axis runs over, the one named last changes fastest.
Arguments:
- tokens: bfloat16 [4096, 2048], P(('dp', 'expert')), may hold values from -6 to 6
- expert_ids: int32 [4096, 2], P(('dp', 'expert')), may hold values from 0 to 7, all different within a row; in each aligned block of 128 rows (0 to 127, 128 to 255, ...) at most 40 rows name the same one
- gate_units: int32 [4096, 2], P(('dp', 'expert')), may hold values from 64 to 1023
- capacity: int32 [8], replicated, may hold values from 512 to 1535
- w_gate: bfloat16 [8, 2048, 1408], P('expert', None, 'dp'), may hold values from -0.125 to 0.125
- w_up: bfloat16 [8, 2048, 1408], P('expert', None, 'dp'), may hold values from -0.125 to 0.125
- w_down: bfloat16 [8, 2048, 1408], P('expert', None, 'dp'), may hold values from -0.15625 to 0.15625
Outputs:
- mixed: bfloat16 [4096, 2048], P(('dp', 'expert'))
Inputs may be any that keep to these rules, and one draw needn't show every extreme that they name: `expert_ids`: each row names two different experts; of one device's 128 rows (aligned blocks) no expert is named more than 40 times.
All inputs are finite; a program needn't handle non-finite values.
Results may differ from a plain program's by a relative error of at most 0.0057.
Values may be sent and summed in bfloat16 or wider, within the bound.
No kernel may reach another device: no remote copies, remote signals or barrier semaphores. Data moves between devices by JAX's collectives and lax.ppermute only.
A program may use at most 128 MiB of HBM per device.

v0:
```python
import jax
import jax.numpy as jnp
from jax import lax
from jax.sharding import PartitionSpec as P


def prefix(shard, axis, combine, identity):
    length, here = (lax.axis_size(axis), lax.axis_index(axis))
    everything = lax.all_gather(shard, axis)
    start = jnp.broadcast_to(jnp.asarray(identity, shard.dtype), shard.shape)

    def step(k, before):
        reached = k < here
        new = combine(before, everything[k])
        return jnp.where(reached, new, before)

    return lax.fori_loop(0, length, step, start)


def expert_rows(rows, gate_w, up_w, down_w):
    gate = jnp.dot(rows, gate_w, preferred_element_type=jnp.float32)
    up = jnp.dot(rows, up_w, preferred_element_type=jnp.float32)
    hidden = (jax.nn.silu(gate) * up).astype(jnp.bfloat16)
    return lax.dot_general(
        hidden, down_w, (((1,), (1,)), ((), ())), preferred_element_type=jnp.float32
    )


def add_counts(earlier, later):
    return earlier + later


def local(tokens, expert_ids, gate_units, capacity, w_gate, w_up, w_down):
    tok_rows = tokens.shape[0]
    width = tokens.shape[1]
    n_experts = capacity.shape[0]
    most = max(2, 5 * tok_rows // (2 * n_experts))
    slots_all = n_experts * most
    flat = expert_ids.reshape(-1)
    onehot = (flat[:, None] == jnp.arange(n_experts, dtype=jnp.int32)[None, :]).astype(jnp.int32)
    local_rank = jnp.sum((jnp.cumsum(onehot, axis=0) - onehot) * onehot, axis=1)
    counts = jnp.sum(onehot, axis=0)
    offsets = prefix(counts, ("dp", "expert"), add_counts, jnp.zeros_like(counts))
    global_slot = jnp.sum(onehot * offsets[None, :], axis=1) + local_rank
    limit = jnp.sum(onehot * capacity[None, :], axis=1)
    kept = global_slot < limit
    weight = jnp.where(kept, gate_units.reshape(-1).astype(jnp.float32) / 1024.0, jnp.float32(0.0))
    send_slot = flat * most + local_rank
    chosen = (send_slot[None, :] == jnp.arange(slots_all, dtype=jnp.int32)[:, None]) & kept[None, :]
    placing = jnp.sum(chosen.reshape(slots_all, tok_rows, 2).astype(jnp.int32), axis=2).astype(
        jnp.bfloat16
    )
    outgoing = jnp.dot(placing, tokens, preferred_element_type=jnp.float32).astype(jnp.bfloat16)
    outgoing = outgoing.reshape(n_experts, most, width)
    arrived = lax.all_to_all(outgoing, "expert", split_axis=0, concat_axis=0, tiled=True).reshape(
        slots_all, width
    )
    produced = expert_rows(
        arrived,
        lax.all_gather(w_gate, "dp", axis=2, tiled=True)[0],
        lax.all_gather(w_up, "dp", axis=2, tiled=True)[0],
        lax.all_gather(w_down, "dp", axis=2, tiled=True)[0],
    )
    answer = produced.astype(jnp.bfloat16).reshape(n_experts, most, width)
    back = lax.all_to_all(answer, "expert", split_axis=0, concat_axis=0, tiled=True).reshape(
        slots_all, width
    )
    picked = back[send_slot].astype(jnp.float32) * weight[:, None]
    mixed = jnp.sum(picked.reshape(tok_rows, 2, width), axis=1)
    return mixed.astype(jnp.bfloat16)


def solution(mesh):
    return jax.shard_map(
        local,
        mesh=mesh,
        in_specs=(
            P(("dp", "expert"), None),
            P(("dp", "expert"), None),
            P(("dp", "expert"), None),
            P(),
            P("expert", None, "dp"),
            P("expert", None, "dp"),
            P("expert", None, "dp"),
        ),
        out_specs=P(("dp", "expert"), None),
        check_vma=False,
    )
```

profile of v0, /device:TPU:0, one launch (start us, length us, event | category | flops | bytes accessed | tf_op | source)
XLA Modules:
  0.0 275.7 jit_solution(2728513415111079550)
XLA Ops:
  6.5 0.0 copy-start
  6.5 0.0 all-gather.5.cloned.1.call-start
  6.5 0.7 all-gather.5.cloned.1.call-update
  7.3 0.0 copy-start.1
  7.3 0.0 copy-start.3
  7.3 0.0 copy-start.2
  7.3 0.0 all-gather.7.cloned.1.call-start
  7.3 0.7 all-gather.7.cloned.1.call-update
  8.0 0.0 all-gather.9.cloned.1.call-start
  8.1 0.7 all-gather.9.cloned.1.call-update
  8.8 0.0 copy-done.1
  8.8 0.1 copy.23
  8.9 0.1 eq.39
  9.1 0.1 eq.43
  9.2 0.1 convert_reduce_fusion.1
  9.3 0.2 dynamic-update-slice
  9.6 42.6 %all-reduce = s32[256]{0:T(256)S(1)} all-reduce(s32[256]{0:T(256)S(1)} %dynamic-update-slice), channel_id=2, replica_groups=mesh['dp'=4,'expert'=8] {'dp','expert'}, use_global_device_ids=true, to_apply=%add | all-reduce | flops 256 | bytes 2048
  52.1 0.1 reshape.134
  52.2 0.6 reduce-window.6
  52.8 0.2 slice_reduce_fusion
  53.1 1.3 while.14
  54.4 0.0 copy-done.3
  54.4 0.1 select_reduce_fusion.1
  54.5 0.1 reduce_sum.63
  54.6 0.1 copy.28
  54.7 0.2 reduce_sum.66
  54.8 0.1 copy.27
  54.9 0.2 reduce_sum.68
  55.1 0.1 copy.29
  55.2 0.1 copy.26
  55.2 0.0 copy-done.2
  55.3 0.0 copy-done
  55.3 0.5 convolution_convert_fusion
  55.8 35.6 %all_to_all.10 = bf16[8,40,2048]{2,1,0:T(8,128)(2,1)S(1)} all-to-all(bf16[8,40,2048]{2,1,0:T(8,128)(2,1)S(1)} %bitcast.35), channel_id=1, replica_groups=mesh['dp'=4,'expert'=8] {'expert'}, dimensions={0} | all-to-all | bytes 2621440 | tf_op jit(solution)/shard_map/all_to_all | solution.py:55
  91.4 0.0 all-gather.5.cloned.1.call-done
  91.4 6.1 %fusion.4 = f32[320,1408]{1,0:T(8,128)} fusion(bf16[320,2048]{1,0:T(8,128)(2,1)S(1)} %bitcast.36, bf16[1,2048,1408]{1,2,0:T(8,128)(2,1)} %all-gather.5.cloned.1.call-done), kind=kOutput, calls=%fused_computation.7 | convolution fusion | flops 1845493760 | bytes 8880128 | tf_op jit(solution)/shard_map/dot_general | solution.py:21
  97.5 48.3 %all-gather.7.cloned.1.call-done = bf16[1,2048,1408]{1,2,0:T(8,128)(2,1)} async-done(((bf16[1,2048,352]{1,2,0:T(8,128)(2,1)}), bf16[1,2048,1408]{1,2,0:T(8,128)(2,1)}) %all-gather.7.cloned.1.call-update) | async-done | bytes 5767184 | tf_op jit(solution)/shard_map/all_gather | solution.py:61
  145.8 67.5 %all-gather.9.cloned.1.call-done = bf16[1,2048,1408]{1,2,0:T(8,128)(2,1)} async-done(((bf16[1,2048,352]{1,2,0:T(8,128)(2,1)}), bf16[1,2048,1408]{1,2,0:T(8,128)(2,1)}) %all-gather.9.cloned.1.call-update) | async-done | bytes 5767184 | tf_op jit(solution)/shard_map/all_gather | solution.py:62
  213.4 10.3 %fusion.9 = bf16[320,2048]{1,0:T(8,128)(2,1)} fusion(bf16[1,2048,1408]{1,2,0:T(8,128)(2,1)} %all-gather.9.cloned.1.call-done, bf16[320,2048]{1,0:T(8,128)(2,1)S(1)} %bitcast.37, bf16[1,2048,1408]{1,2,0:T(8,128)(2,1)} %all-gather.7.cloned.1.call-done, f32[320,1408]{1,0:T(8,128)} %fusion.4), kind=kOutput, calls=%fused_computation.10 | convolution fusion | flops 3694346240 | bytes 15958016 | tf_op jit(solution)/shard_map/dot_general | solution.py:24
  223.7 4.6 %all-to-all-start.1 = ((bf16[8,40,2048]{2,1,0:T(8,128)(2,1)}), bf16[8,40,2048]{2,1,0:T(8,128)(2,1)S(1)}, u32[]{:S(2)}, u32[]{:S(2)}) async-start(bf16[8,40,2048]{2,1,0:T(8,128)(2,1)} %bitcast.7), calls=%async_computation.1 | async-start | bytes 2621440 | tf_op jit(solution)/shard_map/all_to_all | solution.py:65
  228.3 0.1 mul.68
  228.4 0.1 copy.30
  228.5 31.9 %all-to-all-done.1 = bf16[8,40,2048]{2,1,0:T(8,128)(2,1)S(1)} async-done(((bf16[8,40,2048]{2,1,0:T(8,128)(2,1)}), bf16[8,40,2048]{2,1,0:T(8,128)(2,1)S(1)}, u32[]{:S(2)}, u32[]{:S(2)}) %all-to-all-start.1) | async-done | bytes 1310752 | tf_op jit(solution)/shard_map/all_to_all | solution.py:65
  260.5 2.3 gather_fusion
  262.8 2.4 reshape.125
  265.2 4.0 %multiply_reduce_fusion = bf16[128,2048]{1,0:T(8,128)(2,1)} fusion(f32[128,2,2048]{2,1,0:T(2,128)S(1)} %reshape.125, f32[128,2]{1,0:T(8,128)S(1)} %copy.30), kind=kLoop, calls=%fused_computation.13 | loop fusion | flops 786432 | bytes 2622464 | tf_op jit(solution)/shard_map/reduce_sum | solution.py:69
  (42 shorter events, 0.7 us)
Async XLA Ops:
  6.5 48.8 %copy-start = (bf16[128,2048]{1,0:T(8,128)(2,1)S(1)}, bf16[128,2048]{1,0:T(8,128)(2,1)}, u32[]{:S(2)}) copy-start(bf16[128,2048]{1,0:T(8,128)(2,1)} %param.9) | copy-start | bytes 1572868
  6.5 84.9 %all-gather.5.cloned.1.call-start = ((), (), s32[]{:S(2)}) async-start(), calls=%async_computation.2 | async-start | bytes 7208960 | tf_op jit(solution)/shard_map/all_gather | solution.py:60
  7.3 1.5 copy-start.1
  7.3 47.1 %copy-start.3 = (s32[8]{0:T(128)S(1)}, s32[8]{0:T(128)}, u32[]{:S(2)}) copy-start(s32[8]{0:T(128)} %param.12) | copy-start | bytes 100
  7.3 47.9 %copy-start.2 = (s32[128,2]{0,1:T(2,128)S(1)}, s32[128,2]{0,1:T(2,128)}, u32[]{:S(2)}) copy-start(s32[128,2]{0,1:T(2,128)} %param.11) | copy-start | bytes 3076
  7.3 138.6 %all-gather.7.cloned.1.call-start = ((), (), s32[]{:S(2)}) async-start(), calls=%async_computation.3 | async-start | bytes 7208960 | tf_op jit(solution)/shard_map/all_gather | solution.py:61
  8.0 205.4 %all-gather.9.cloned.1.call-start = ((), (), s32[]{:S(2)}) async-start(), calls=%async_computation.4 | async-start | bytes 7208960 | tf_op jit(solution)/shard_map/all_gather | solution.py:62
  223.7 36.8 %all-to-all-start.1 = ((bf16[8,40,2048]{2,1,0:T(8,128)(2,1)}), bf16[8,40,2048]{2,1,0:T(8,128)(2,1)S(1)}, u32[]{:S(2)}, u32[]{:S(2)}) async-start(bf16[8,40,2048]{2,1,0:T(8,128)(2,1)} %bitcast.7), calls=%async_computation.1 | async-start | bytes 2621440 | tf_op jit(solution)/shard_map/all_to_all | solution.py:65
Sparse Core Ops, SparseCore 0:
  9.2 69.0 all-gather.4
  80.1 65.6 all-gather.6
  147.7 65.6 all-gather.8
where the time goes:
time: 276 us
  waiting for transfers between devices  150 us (54%)
  blocking collectives  78.1 us (28%)
  matrix products  16.9 us (6%)
  between operations  13.3 us (5%)
  local copies, waits for them, and re-layouts  6.6 us (2%)
  other arithmetic  5.55 us (2%)
  starting transfers between devices  4.68 us (2%)
    all_gather x1, waiting for transfers between devices, local(): lax.all_gather(w_down, 'dp', axis=2, tiled=True)[0]  67.5 us
    all_gather x1, waiting for transfers between devices, local(): lax.all_gather(w_up, 'dp', axis=2, tiled=True)[0]  48.3 us
    unnamed x1, blocking collectives  42.6 us
    all_to_all x1, blocking collectives, local(): lax.all_to_all(outgoing, 'expert', split_axis=0, concat_axis=0, tiled=True)  35.6 us
    all_to_all x1, waiting for transfers between devices, local(): lax.all_to_all(answer, 'expert', split_axis=0, concat_axis=0, tiled=True)  31.9 us
    dot_general x1, matrix products, expert_rows(): lax.dot_general(hidden, down_w, (((1,), (1,)), ((), ())), preferred_eleme...  10.3 us
    dot_general x1, matrix products, expert_rows(): gate = jnp.dot(rows, gate_w, preferred_element_type=jnp.float32)  6.11 us
  transfers between devices with their start and end apart: 4, of which 3 were waited for; matrix products, arithmetic and copies ran while one was open for 4% of the time, Pallas kernels for 0%

commit v1 on v0

--- a/solution.py
+++ b/solution.py
@@ -2,6 +2,28 @@
 import jax.numpy as jnp
 from jax import lax
 from jax.sharding import PartitionSpec as P
+
+
+def in_blocks(array, dim, peers):
+    before, after = (array.shape[:dim], array.shape[dim + 1 :])
+    return jnp.moveaxis(array.reshape(*before, peers, -1, *after), dim, 0)
+
+
+def in_order(tiles, dim):
+    tiles = jnp.moveaxis(tiles, 0, dim)
+    dims = tiles.shape
+    return tiles.reshape(*dims[:dim], dims[dim] * dims[dim + 1], *dims[dim + 2 :])
+
+
+def rotated_exchange(x, axis, split_dim, concat_dim):
+    size, here = (lax.axis_size(axis), lax.axis_index(axis))
+    blocks = in_blocks(x, split_dim, size)
+    done = [blocks[here]]
+    for step in range(1, size):
+        sent = blocks[(here + step) % size]
+        done.append(lax.ppermute(sent, axis, [(i, (i + step) % size) for i in range(size)]))
+    blocks = jnp.stack(done)[(here - jnp.arange(size)) % size]
+    return in_order(blocks, concat_dim)
 
 
 def prefix(shard, axis, combine, identity):
@@ -62,9 +84,7 @@
         lax.all_gather(w_down, "dp", axis=2, tiled=True)[0],
     )
     answer = produced.astype(jnp.bfloat16).reshape(n_experts, most, width)
-    back = lax.all_to_all(answer, "expert", split_axis=0, concat_axis=0, tiled=True).reshape(
-        slots_all, width
-    )
+    back = rotated_exchange(answer, "expert", 0, 0).reshape(slots_all, width)
     picked = back[send_slot].astype(jnp.float32) * weight[:, None]
     mixed = jnp.sum(picked.reshape(tok_rows, 2, width), axis=1)
     return mixed.astype(jnp.bfloat16)

time: 276 us -> 270 us (0.978)
  the two profiles are of different devices: /device:TPU:0 before, /device:TPU:9 now
where the time goes in v1:
time: 270 us
  waiting for transfers between devices  172 us (64%)
  blocking collectives  41.2 us (15%)
  matrix products  17.3 us (6%)
  between operations  13.4 us (5%)
  starting transfers between devices  11.8 us (4%)
  local copies, waits for them, and re-layouts  8.23 us (3%)
  other arithmetic  5.46 us (2%)
    all_gather x1, waiting for transfers between devices, local(): lax.all_gather(w_down, 'dp', axis=2, tiled=True)[0]  67.5 us
    all_gather x1, waiting for transfers between devices, local(): lax.all_gather(w_up, 'dp', axis=2, tiled=True)[0]  49.2 us
    unnamed x1, blocking collectives  41.2 us
    all_to_all x1, waiting for transfers between devices, local(): lax.all_to_all(outgoing, 'expert', split_axis=0, concat_axis=0, tiled=True)  28.5 us
    ppermute x7, waiting for transfers between devices, rotated_exchange(): lax.ppermute(sent, axis, [(i, (i + step) % size) for i in range(size)])  24.6 us
    dot_general x1, matrix products, expert_rows(): lax.dot_general(hidden, down_w, (((1,), (1,)), ((), ())), preferred_eleme...  9.19 us
    ppermute x7, starting transfers between devices, rotated_exchange(): lax.ppermute(sent, axis, [(i, (i + step) % size) for i in range(size)])  7.52 us
    dot_general x1, matrix products, expert_rows(): gate = jnp.dot(rows, gate_w, preferred_element_type=jnp.float32)  6.5 us
  transfers between devices with their start and end apart: 11, of which 8 were waited for; matrix products, arithmetic and copies ran while one was open for 4% of the time, Pallas kernels for 0%

profile of v1, /device:TPU:9, one launch (start us, length us, event | category | flops | bytes accessed | tf_op | source)
XLA Modules:
  0.0 270.0 jit_solution(2825350137911415098)
XLA Ops:
  6.5 0.7 all-gather.5.cloned.1.call-update
  7.3 0.0 all-gather.7.cloned.1.call-start
  7.3 0.7 all-gather.7.cloned.1.call-update
  8.0 0.0 all-gather.9.cloned.1.call-start
  8.1 0.7 all-gather.9.cloned.1.call-update
  8.8 0.1 copy.23
  8.9 0.1 eq.49
  9.1 0.1 eq.53
  9.2 0.1 convert_reduce_fusion.1
  9.3 0.2 dynamic-update-slice
  9.6 41.2 %all-reduce = s32[256]{0:T(256)S(1)} all-reduce(s32[256]{0:T(256)S(1)} %dynamic-update-slice), channel_id=2, replica_groups=mesh['dp'=4,'expert'=8] {'dp','expert'}, use_global_device_ids=true, to_apply=%add | all-reduce | flops 256 | bytes 2048
  50.8 0.1 reshape.185
  50.9 0.6 reduce-window.6
  51.5 0.2 slice_reduce_fusion
  51.7 1.3 while.14
  53.0 0.1 select_reduce_fusion.1
  53.1 0.1 reduce_sum.63
  53.3 0.1 copy.28
  53.3 0.2 reduce_sum.66
  53.5 0.1 copy.27
  53.5 0.2 reduce_sum.68
  53.7 0.1 copy.29
  53.8 0.1 copy.26
  54.0 1.6 convolution_convert_fusion
  55.5 4.2 %all-to-all-start = ((bf16[8,40,2048]{2,1,0:T(8,128)(2,1)}), bf16[8,40,2048]{2,1,0:T(8,128)(2,1)S(1)}, u32[]{:S(2)}, u32[]{:S(2)}) async-start(bf16[8,40,2048]{2,1,0:T(8,128)(2,1)} %bitcast.2), calls=%async_computation | async-start | bytes 2621440 | tf_op jit(solution)/shard_map/all_to_all | solution.py:77
  59.8 0.1 mul.68
  60.0 28.5 %all-to-all-done = bf16[8,40,2048]{2,1,0:T(8,128)(2,1)S(1)} async-done(((bf16[8,40,2048]{2,1,0:T(8,128)(2,1)}), bf16[8,40,2048]{2,1,0:T(8,128)(2,1)S(1)}, u32[]{:S(2)}, u32[]{:S(2)}) %all-to-all-start) | async-done | bytes 1310752 | tf_op jit(solution)/shard_map/all_to_all | solution.py:77
  88.4 6.5 %fusion.4 = f32[320,1408]{1,0:T(8,128)} fusion(bf16[320,2048]{1,0:T(8,128)(2,1)S(1)} %bitcast.67, bf16[1,2048,1408]{1,2,0:T(8,128)(2,1)} %all-gather.5.cloned.1.call-done), kind=kOutput, calls=%fused_computation.8 | convolution fusion | flops 1845493760 | bytes 8880128 | tf_op jit(solution)/shard_map/dot_general | solution.py:43
  94.9 49.2 %all-gather.7.cloned.1.call-done = bf16[1,2048,1408]{1,2,0:T(8,128)(2,1)} async-done(((bf16[1,2048,352]{1,2,0:T(8,128)(2,1)}), bf16[1,2048,1408]{1,2,0:T(8,128)(2,1)}) %all-gather.7.cloned.1.call-update) | async-done | bytes 5767184 | tf_op jit(solution)/shard_map/all_gather | solution.py:83
  144.1 67.5 %all-gather.9.cloned.1.call-done = bf16[1,2048,1408]{1,2,0:T(8,128)(2,1)} async-done(((bf16[1,2048,352]{1,2,0:T(8,128)(2,1)}), bf16[1,2048,1408]{1,2,0:T(8,128)(2,1)}) %all-gather.9.cloned.1.call-update) | async-done | bytes 5767184 | tf_op jit(solution)/shard_map/all_gather | solution.py:84
  211.7 9.2 %fusion.9 = bf16[320,2048]{1,0:T(8,128)(2,1)S(1)} fusion(bf16[1,2048,1408]{1,2,0:T(8,128)(2,1)} %all-gather.9.cloned.1.call-done, bf16[320,2048]{1,0:T(8,128)(2,1)S(1)} %bitcast.68, bf16[1,2048,1408]{1,2,0:T(8,128)(2,1)} %all-gather.7.cloned.1.call-done, f32[320,1408]{1,0:T(8,128)} %fusion.4), kind=kOutput, calls=%fused_computation.11 | convolution fusion | flops 3694346240 | bytes 15958016 | tf_op jit(solution)/shard_map/dot_general | solution.py:46
  220.9 0.9 dynamic-slice_bitcast_fusion
  221.8 1.9 collective-permute-start
  223.7 0.1 copy.30
  223.8 1.3 collective-permute-start.1
  225.1 0.2 collective-permute-start.2
  225.3 1.2 collective-permute-start.3
  226.5 1.7 collective-permute-start.4
  228.3 1.2 collective-permute-start.5
  229.4 2.0 collective-permute-done.1
  231.4 16.9 %collective-permute-done.2 = bf16[1,40,2048]{2,1,0:T(8,128)(2,1)S(1)} collective-permute-done((bf16[1,40,2048]{2,1,0:T(8,128)(2,1)}, bf16[1,40,2048]{2,1,0:T(8,128)(2,1)S(1)}, u32[]{:S(2)}, u32[]{:S(2)}) %collective-permute-start.2) | collective-permute-done | bytes 163872 | tf_op jit(solution)/shard_map/ppermute | solution.py:24
  248.4 3.5 %collective-permute-done.3 = bf16[1,40,2048]{2,1,0:T(8,128)(2,1)S(1)} collective-permute-done((bf16[1,40,2048]{2,1,0:T(8,128)(2,1)}, bf16[1,40,2048]{2,1,0:T(8,128)(2,1)S(1)}, u32[]{:S(2)}, u32[]{:S(2)}) %collective-permute-start.3) | collective-permute-done | bytes 163872 | tf_op jit(solution)/shard_map/ppermute | solution.py:24
  251.9 2.1 collective-permute-done.5
  254.0 0.1 collective-permute-done.6
  254.1 0.6 gather_fusion
  254.8 2.3 gather_fusion.1
  257.1 2.4 reshape.166
  259.5 3.9 %multiply_reduce_fusion = bf16[128,2048]{1,0:T(8,128)(2,1)} fusion(f32[128,2,2048]{2,1,0:T(2,128)S(1)} %reshape.166, f32[128,2]{1,0:T(8,128)S(1)} %copy.30), kind=kLoop, calls=%fused_computation.14 | loop fusion | flops 786432 | bytes 2622464 | tf_op jit(solution)/shard_map/reduce_sum | solution.py:89
  (64 shorter events, 0.9 us)
Async XLA Ops:
  6.5 47.4 %copy-start = (bf16[128,2048]{1,0:T(8,128)(2,1)S(1)}, bf16[128,2048]{1,0:T(8,128)(2,1)}, u32[]{:S(2)}) copy-start(bf16[128,2048]{1,0:T(8,128)(2,1)} %param.9) | copy-start | bytes 1572868
  6.5 81.9 %all-gather.5.cloned.1.call-start = ((), (), s32[]{:S(2)}) async-start(), calls=%async_computation.1 | async-start | bytes 7208960 | tf_op jit(solution)/shard_map/all_gather | solution.py:82
  7.3 1.5 copy-start.1
  7.3 45.8 %copy-start.3 = (s32[8]{0:T(128)S(1)}, s32[8]{0:T(128)}, u32[]{:S(2)}) copy-start(s32[8]{0:T(128)} %param.12) | copy-start | bytes 100
  7.3 136.8 %all-gather.7.cloned.1.call-start = ((), (), s32[]{:S(2)}) async-start(), calls=%async_computation.2 | async-start | bytes 7208960 | tf_op jit(solution)/shard_map/all_gather | solution.py:83
  8.0 45.8 %copy-start.2 = (s32[128,2]{0,1:T(2,128)S(1)}, s32[128,2]{0,1:T(2,128)}, u32[]{:S(2)}) copy-start(s32[128,2]{0,1:T(2,128)} %param.11) | copy-start | bytes 3076
  8.0 203.6 %all-gather.9.cloned.1.call-start = ((), (), s32[]{:S(2)}) async-start(), calls=%async_computation.3 | async-start | bytes 7208960 | tf_op jit(solution)/shard_map/all_gather | solution.py:84
  55.5 32.9 %all-to-all-start = ((bf16[8,40,2048]{2,1,0:T(8,128)(2,1)}), bf16[8,40,2048]{2,1,0:T(8,128)(2,1)S(1)}, u32[]{:S(2)}, u32[]{:S(2)}) async-start(bf16[8,40,2048]{2,1,0:T(8,128)(2,1)} %bitcast.2), calls=%async_computation | async-start | bytes 2621440 | tf_op jit(solution)/shard_map/all_to_all | solution.py:77
  221.8 6.5 %collective-permute-start = (bf16[1,40,2048]{2,1,0:T(8,128)(2,1)}, bf16[1,40,2048]{2,1,0:T(8,128)(2,1)S(1)}, u32[]{:S(2)}, u32[]{:S(2)}) collective-permute-start(bf16[1,40,2048]{2,1,0:T(8,128)(2,1)} %get-tuple-element.119), channel_id=1, source_target_pairs={{0,1},{1,2},{2,3},{3,4},{4,5},{5,6},{6,7},{7,0},{8,9},{9,10},{10,1... | collective-permute-start | bytes 491528 | tf_op jit(solution)/shard_map/ppermute | solution.py:24
  223.8 7.6 %collective-permute-start.1 = (bf16[1,40,2048]{2,1,0:T(8,128)(2,1)}, bf16[1,40,2048]{2,1,0:T(8,128)(2,1)S(1)}, u32[]{:S(2)}, u32[]{:S(2)}) collective-permute-start(bf16[1,40,2048]{2,1,0:T(8,128)(2,1)} %get-tuple-element.118), channel_id=1, source_target_pairs={{0,2},{1,3},{2,4},{3,5},{4,6},{5,7},{6,0},{7,1},{8,10},{9,11},{10,... | collective-permute-start | bytes 491528 | tf_op jit(solution)/shard_map/ppermute | solution.py:24
  225.1 23.3 %collective-permute-start.2 = (bf16[1,40,2048]{2,1,0:T(8,128)(2,1)}, bf16[1,40,2048]{2,1,0:T(8,128)(2,1)S(1)}, u32[]{:S(2)}, u32[]{:S(2)}) collective-permute-start(bf16[1,40,2048]{2,1,0:T(8,128)(2,1)} %get-tuple-element.117), channel_id=1, source_target_pairs={{0,3},{1,4},{2,5},{3,6},{4,7},{5,0},{6,1},{7,2},{8,11},{9,12},{10,... | collective-permute-start | bytes 491528 | tf_op jit(solution)/shard_map/ppermute | solution.py:24
  225.3 26.5 %collective-permute-start.3 = (bf16[1,40,2048]{2,1,0:T(8,128)(2,1)}, bf16[1,40,2048]{2,1,0:T(8,128)(2,1)S(1)}, u32[]{:S(2)}, u32[]{:S(2)}) collective-permute-start(bf16[1,40,2048]{2,1,0:T(8,128)(2,1)} %get-tuple-element.116), channel_id=1, source_target_pairs={{0,4},{1,5},{2,6},{3,7},{4,0},{5,1},{6,2},{7,3},{8,12},{9,13},{10,... | collective-permute-start | bytes 491528 | tf_op jit(solution)/shard_map/ppermute | solution.py:24
  226.5 25.3 %collective-permute-start.4 = (bf16[1,40,2048]{2,1,0:T(8,128)(2,1)}, bf16[1,40,2048]{2,1,0:T(8,128)(2,1)S(1)}, u32[]{:S(2)}, u32[]{:S(2)}) collective-permute-start(bf16[1,40,2048]{2,1,0:T(8,128)(2,1)} %get-tuple-element.115), channel_id=1, source_target_pairs={{0,5},{1,6},{2,7},{3,0},{4,1},{5,2},{6,3},{7,4},{8,13},{9,14},{10,... | collective-permute-start | bytes 491528 | tf_op jit(solution)/shard_map/ppermute | solution.py:24
  228.3 25.8 %collective-permute-start.5 = (bf16[1,40,2048]{2,1,0:T(8,128)(2,1)S(1)}, bf16[1,40,2048]{2,1,0:T(8,128)(2,1)S(1)}, u32[]{:S(2)}, u32[]{:S(2)}) collective-permute-start(bf16[1,40,2048]{2,1,0:T(8,128)(2,1)S(1)} %get-tuple-element.114), channel_id=1, source_target_pairs={{0,6},{1,7},{2,0},{3,1},{4,2},{5,3},{6,4},{7,5},{8,14},{9,15},{10,... | collective-permute-start | bytes 491528 | tf_op jit(solution)/shard_map/ppermute | solution.py:24
  231.4 22.7 %collective-permute-start.6 = (bf16[1,40,2048]{2,1,0:T(8,128)(2,1)S(1)}, bf16[1,40,2048]{2,1,0:T(8,128)(2,1)S(1)}, u32[]{:S(2)}, u32[]{:S(2)}) collective-permute-start(bf16[1,40,2048]{2,1,0:T(8,128)(2,1)S(1)} %get-tuple-element.113), channel_id=1, source_target_pairs={{0,7},{1,0},{2,1},{3,2},{4,3},{5,4},{6,5},{7,6},{8,15},{9,8},{10,9... | collective-permute-start | bytes 491528 | tf_op jit(solution)/shard_map/ppermute | solution.py:24
Sparse Core Ops, SparseCore 0:
  9.2 67.3 all-gather.4
  78.4 65.6 all-gather.6
  146.0 65.6 all-gather.8
